TPU v7x, 256 devices: a whole 4x4x8 slice. The times are simulated.
256 devices in a mesh: section: 2 (over x_hi), feat: 16 (over y, x_lo, core), width: 8 (over z).
Axes of the slice: x: 4 (x_hi: 2, x_lo: 2; x = x_hi * 2 + x_lo), y: 4, z: 8, core: 2. Of those that a mesh axis runs over, the one named last changes fastest.
Arguments:
- mlp_inputs: bfloat16 [4, 1024, 2304], P('section', 'width'), may hold values from -6 to 6
- encoder: bfloat16 [4, 2304, 16384], P('section', 'width', 'feat'), may hold values from -0.125 to 0.125
- enc_bias: float32 [4, 16384], P('section', 'feat'), may hold values from -3 to 3
- decoder: bfloat16 [10, 16384, 2304], P('section', 'feat', 'width'), may hold values from -0.046875 to 0.046875
- dec_bias: float32 [4, 2304], P(None, 'width'), may hold values from -3 to 3
- targets: bfloat16 [4, 1024, 2304], P(None, None, 'width'), may hold values from -6 to 6
- live_rows: int32 [1024], replicated, may hold values 0 or 1
Outputs:
- errors: bfloat16 [4, 1024, 2304], P(None, None, 'width')
- gradients: bfloat16 [10, 16384, 2304], P('section', 'feat', 'width')
All inputs are finite; a program needn't handle non-finite values.
Results may differ from a plain program's by a relative error of at most 0.0042.
Values may be sent and summed in bfloat16 or wider, within the bound.
No kernel may reach another device: no remote copies, remote signals or barrier semaphores. Data moves between devices by JAX's collectives and lax.ppermute only.
A program may use at most 128 MiB of HBM per device.

v0:
```python
import jax
import jax.numpy as jnp
from jax import lax
from jax.sharding import PartitionSpec as P


def from_behind(value, axis, steps):
    count = lax.axis_size(axis)
    initial, last = (max(0, -steps), min(count, count - steps))
    return lax.ppermute(value, axis, [(source, source + steps) for source in range(initial, last)])


def pair_tables(layer_count):
    source_ids = []
    target_ids = []
    for source in range(layer_count):
        for target in range(source, layer_count):
            source_ids.append(source)
            target_ids.append(target)
    return (jnp.array(source_ids, jnp.int32), jnp.array(target_ids, jnp.int32))


def local(mlp_inputs, encoder, enc_bias, decoder, dec_bias, targets, live_rows):
    layers_here, tok_local, model_width = mlp_inputs.shape
    pre_act = jnp.einsum(
        "ltd,ldf->tlf",
        mlp_inputs,
        lax.all_gather(encoder, "width", axis=1, tiled=True),
        preferred_element_type=jnp.float32,
    )
    local_feats = jnp.maximum(pre_act + enc_bias[None, :, :], 0.0).astype(jnp.bfloat16)
    token_feats = lax.all_gather(local_feats, "width", axis=0, tiled=True)
    layers_all = dec_bias.shape[0]
    tokens_all = live_rows.shape[0]
    per_section = decoder.shape[0]
    source_ids, target_ids = pair_tables(layers_all)
    section_id = lax.axis_index("section")
    earlier = from_behind(token_feats[:, layers_here - 1], "section", 1)
    features = jnp.concatenate([earlier[:, None, :], token_feats], axis=1)
    first_layer = section_id * layers_here - 1
    rebuilt = jnp.zeros((layers_all, tokens_all, decoder.shape[2]), jnp.float32)
    chosen = []
    for pair_slot in range(per_section):
        pair_id = section_id * per_section + pair_slot
        source = source_ids[pair_id]
        target = target_ids[pair_id]
        picked = lax.dynamic_index_in_dim(features, source - first_layer, 1, keepdims=False)
        chosen.append((picked, target))
        partial_value = jnp.dot(picked, decoder[pair_slot], preferred_element_type=jnp.float32)
        current = lax.dynamic_index_in_dim(rebuilt, target, 0, keepdims=False)
        rebuilt = lax.dynamic_update_index_in_dim(rebuilt, current + partial_value, target, 0)
    summed = lax.psum(rebuilt, ("section", "feat"))
    keep_rows = live_rows.astype(jnp.float32)[None, :, None]
    errors = ((summed + dec_bias[:, None, :] - targets.astype(jnp.float32)) * keep_rows).astype(
        jnp.bfloat16
    )
    gradients = []
    for picked, target in chosen:
        residual = lax.dynamic_index_in_dim(errors, target, 0, keepdims=False)
        product = lax.dot_general(
            picked, residual, (((0,), (0,)), ((), ())), preferred_element_type=jnp.float32
        )
        gradients.append((product / tokens_all).astype(jnp.bfloat16))
    return (errors, jnp.stack(gradients))


def solution(mesh):
    placed = (
        P("section", "width", None),
        P("section", "width", "feat"),
        P("section", "feat"),
        P("section", "feat", "width"),
        P(None, "width"),
        P(None, None, "width"),
        P(),
    )
    return jax.shard_map(
        local,
        mesh=mesh,
        in_specs=placed,
        out_specs=(P(None, None, "width"), P("section", "feat", "width")),
        check_vma=False,
    )
```

profile of v0, /device:TPU:1, one launch (start us, length us, event | category | flops | bytes accessed | tf_op | source)
XLA Modules:
  0.0 397.8 jit_solution(8431505922366384273)
XLA Ops:
  7.2 0.0 copy-start
  7.2 0.0 all-gather.3.cloned.1.call-start
  7.2 0.7 all-gather.3.cloned.1.call-update
  7.9 0.0 all-gather.5.cloned.1.call-start
  8.0 109.4 %all-gather.3.cloned.1.call-done = bf16[2,2304,1024]{2,1,0:T(8,128)(2,1)} async-done(((bf16[2,288,1024]{2,1,0:T(8,128)(2,1)}), bf16[2,2304,1024]{2,1,0:T(8,128)(2,1)}) %all-gather.3.cloned.1.call-update) | async-done | bytes 9437200 | tf_op jit(solution)/shard_map/all_gather | solution.py:28
  117.3 0.0 copy-done
  117.3 7.3 %fusion.36 = bf16[128,2,1024]{0,2,1:T(8,128)(2,1)} fusion(bf16[2,2304,1024]{2,1,0:T(8,128)(2,1)} %all-gather.3.cloned.1.call-done, bf16[2,128,2304]{2,1,0:T(8,128)(2,1)S(1)} %copy-done, f32[2,1024]{1,0:T(2,128)} %param.11), kind=kOutput, calls=%fused_computation.59 | convolution fusion | flops 1208745984 | bytes 11149312 | tf_op jit(solution)/shard_map/ltd,ldf->tlf/dot_general | solution.py:25
  124.7 0.0 copy-start.5
  124.7 0.0 copy-start.6
  124.7 0.0 all-gather.5.cloned.1.call-update
  124.7 0.0 all-reduce.2.cloned.1.call-start
  124.7 57.6 %all-gather.5.cloned.1.call-done = bf16[1024,2,1024]{0,2,1:T(8,128)(2,1)} async-done(((bf16[128,2,1024]{0,2,1:T(8,128)(2,1)}), bf16[1024,2,1024]{0,2,1:T(8,128)(2,1)}) %all-gather.5.cloned.1.call-update) | async-done | bytes 4194320 | tf_op jit(solution)/shard_map/all_gather | solution.py:32
  182.4 3.1 slice_bitcast_fusion
  185.4 4.4 %collective-permute-start = (bf16[1024,1024]{0,1:T(8,128)(2,1)}, bf16[1024,1024]{0,1:T(8,128)(2,1)S(1)}, u32[]{:S(2)}, u32[]{:S(2)}) collective-permute-start(bf16[1024,1024]{0,1:T(8,128)(2,1)} %slice_bitcast_fusion), channel_id=1, source_target_pairs={{0,128},{1,129},{2,130},{3,131},{4,132},{5,133},{6,134},{7,135},{8... | collective-permute-start | bytes 6291464 | tf_op jit(solution)/shard_map/ppermute | solution.py:10
  189.9 0.0 copy-done.5
  189.9 0.0 copy-done.6
  189.9 0.7 fusion.72
  203.2 26.7 %collective-permute-done = bf16[1024,1024]{0,1:T(8,128)(2,1)S(1)} collective-permute-done((bf16[1024,1024]{0,1:T(8,128)(2,1)}, bf16[1024,1024]{0,1:T(8,128)(2,1)S(1)}, u32[]{:S(2)}, u32[]{:S(2)}) %collective-permute-start) | collective-permute-done | bytes 2097184 | tf_op jit(solution)/shard_map/ppermute | solution.py:10
  229.9 0.0 copy-start.1
  229.9 3.0 broadcast_in_dim.25
  232.9 0.8 copy-done.1
  233.7 0.0 copy-start.3
  233.7 3.4 fusion.18
  237.1 1.3 constant_dynamic-slice_fusion.3
  238.5 0.0 copy-done.3
  238.5 2.2 fusion.17
  240.7 1.3 constant_dynamic-slice_fusion.2
  242.1 2.2 fusion.15
  244.3 1.3 constant_dynamic-slice_fusion.1
  245.6 2.3 fusion.13
  247.9 1.3 constant_dynamic-slice_fusion
  249.3 2.2 fusion.11
  251.5 0.0 copy-start.8
  251.5 0.0 copy-start.7
  251.5 0.0 all-reduce.2.cloned.1.call-update
  251.5 0.7 copy-done.8
  252.2 126.4 %all-reduce.2.cloned.1.call-done = f32[4,1024,288]{1,2,0:T(8,128)} async-done(((f32[4,1024,288]{1,2,0:T(8,128)}), f32[4,1024,288]{1,2,0:T(8,128)}) %all-reduce.2.cloned.1.call-update) | async-done | bytes 4718608 | tf_op jit(solution)/shard_map/psum | solution.py:52
  378.6 0.0 copy-done.7
  378.6 3.9 multiply_convert_fusion
  382.5 0.3 copy-done.2
  382.8 1.4 fusion.35
  384.2 1.4 fusion.33
  385.6 1.4 fusion.31
  386.9 1.4 fusion.29
  388.3 0.0 copy-done.4
  388.3 1.4 fusion.27
  389.7 0.0 copy-start.9
  389.7 1.6 copy-done.9
  (3 shorter events, 0.0 us)
Async XLA Ops:
  7.2 110.2 %copy-start = (bf16[2,128,2304]{2,1,0:T(8,128)(2,1)S(1)}, bf16[2,128,2304]{2,1,0:T(8,128)(2,1)}, u32[]{:S(2)}) copy-start(bf16[2,128,2304]{2,1,0:T(8,128)(2,1)} %param.9) | copy-start | bytes 3538948
  7.2 110.2 %all-gather.3.cloned.1.call-start = ((), (), s32[]{:S(2)}) async-start(), calls=%async_computation | async-start | bytes 10616832 | tf_op jit(solution)/shard_map/all_gather | solution.py:28
  7.9 174.4 %all-gather.5.cloned.1.call-start = ((), (), s32[]{:S(2)}) async-start(), calls=%async_computation.1 | async-start | bytes 4718592 | tf_op jit(solution)/shard_map/all_gather | solution.py:32
  124.7 65.2 %copy-start.5 = (s32[10]{0:T(128)S(1)}, s32[10]{0:T(128)}, u32[]{:S(2)}) copy-start(s32[10]{0:T(128)} %constant.92.clone) | copy-start | bytes 124
  124.7 65.2 %copy-start.6 = (s32[10]{0:T(128)S(1)}, s32[10]{0:T(128)}, u32[]{:S(2)}) copy-start(s32[10]{0:T(128)} %constant.93.clone) | copy-start | bytes 124
  124.7 253.9 %all-reduce.2.cloned.1.call-start = ((), (), s32[]{:S(2)}) async-start(), calls=%async_computation.2 | async-start | bytes 9437184 | tf_op jit(solution)/shard_map/psum | solution.py:52
  185.4 44.5 %collective-permute-start = (bf16[1024,1024]{0,1:T(8,128)(2,1)}, bf16[1024,1024]{0,1:T(8,128)(2,1)S(1)}, u32[]{:S(2)}, u32[]{:S(2)}) collective-permute-start(bf16[1024,1024]{0,1:T(8,128)(2,1)} %slice_bitcast_fusion), channel_id=1, source_target_pairs={{0,128},{1,129},{2,130},{3,131},{4,132},{5,133},{6,134},{7,135},{8... | collective-permute-start | bytes 6291464 | tf_op jit(solution)/shard_map/ppermute | solution.py:10
  229.9 3.8 copy-start.1
  233.7 4.7 %copy-start.3 = (bf16[5,1024,288]{1,2,0:T(8,128)(2,1)S(1)}, bf16[5,1024,288]{1,2,0:T(8,128)(2,1)}, u32[]{:S(2)}) copy-start(bf16[5,1024,288]{1,2,0:T(8,128)(2,1)} %param.12) | copy-start | bytes 8847364
  251.5 0.7 copy-start.8
  251.5 127.1 %copy-start.7 = (f32[4,288]{1,0:T(4,128)S(1)}, f32[4,288]{1,0:T(4,128)}, u32[]{:S(2)}) copy-start(f32[4,288]{1,0:T(4,128)} %param.13) | copy-start | bytes 13828
  378.6 4.2 %copy-start.2 = (bf16[1024,2,1024]{0,2,1:T(8,128)(2,1)S(1)}, bf16[1024,2,1024]{0,2,1:T(8,128)(2,1)}, u32[]{:S(2)}) copy-start(bf16[1024,2,1024]{0,2,1:T(8,128)(2,1)} %all-gather.5.cloned.1.call-done) | copy-start | bytes 12582916
  382.8 5.5 %copy-start.4 = (bf16[4,1024,288]{1,2,0:T(8,128)(2,1)}, bf16[4,1024,288]{1,2,0:T(8,128)(2,1)S(1)}, u32[]{:S(2)}) copy-start(bf16[4,1024,288]{1,2,0:T(8,128)(2,1)S(1)} %multiply_convert_fusion) | copy-start | bytes 7077892
  389.7 1.6 copy-start.9
Sparse Core Ops, SparseCore 0:
  9.8 107.5 all-gather.2
  124.8 57.5 all-gather.4
  251.6 126.9 all-reduce.1
where the time goes:
time: 398 us
  waiting for transfers between devices  321 us (81%)
  matrix products  26.5 us (7%)
  between operations  26.5 us (7%)
  local copies, waits for them, and re-layouts  15.5 us (4%)
  starting transfers between devices  4.52 us (1%)
    psum x1, waiting for transfers between devices, local(): summed = lax.psum(rebuilt, ('section', 'feat'))  126 us
    all_gather x1, waiting for transfers between devices, local(): lax.all_gather(encoder, 'width', axis=1, tiled=True)  109 us
    all_gather x1, waiting for transfers between devices, local(): token_feats = lax.all_gather(local_feats, 'width', axis=0, tiled=True)  57.6 us
    ppermute x1, waiting for transfers between devices, from_behind(): lax.ppermute(value, axis, [(source, source + steps) for source in range(i...  26.7 us
    dot_general x5, matrix products, local(): jnp.dot(picked, decoder[pair_slot], preferred_element_type=jnp.float32)  12.3 us
  transfers between devices with their start and end apart: 4, of which 4 were waited for; matrix products, arithmetic and copies ran while one was open for 0% of the time, Pallas kernels for 0%

commit v1 on v0

--- a/solution.py
+++ b/solution.py
@@ -2,6 +2,27 @@
 import jax.numpy as jnp
 from jax import lax
 from jax.sharding import PartitionSpec as P
+from jax.lax import axis_index, axis_size, ppermute
+
+
+def report_classes(body, x_part):
+    next_value, now, row_out = (axis_size("width"), axis_index("width"), body.shape[1])
+    buffers = []
+    for tick in range(next_value):
+        buffers.append((tick, (tick + 1) % next_value))
+    lanes = []
+    for tick in range(next_value):
+        lanes.append((tick, (tick - 1) % next_value))
+    block_last = next_value // 2
+    lower = d_next = body
+    z1 = x_part(body, now * row_out)
+    for b in range(1, block_last + 1):
+        lower = ppermute(lower, "width", buffers)
+        if b < next_value - block_last:
+            d_next = ppermute(d_next, "width", lanes)
+            z1 = z1 + x_part(d_next, (now + b) % next_value * row_out)
+        z1 = z1 + x_part(lower, (now - b) % next_value * row_out)
+    return z1
 
 
 def from_behind(value, axis, steps):
@@ -22,11 +43,14 @@
 
 def local(mlp_inputs, encoder, enc_bias, decoder, dec_bias, targets, live_rows):
     layers_here, tok_local, model_width = mlp_inputs.shape
-    pre_act = jnp.einsum(
-        "ltd,ldf->tlf",
-        mlp_inputs,
-        lax.all_gather(encoder, "width", axis=1, tiled=True),
-        preferred_element_type=jnp.float32,
+    pre_act = report_classes(
+        encoder,
+        x_part=lambda part, start: jnp.einsum(
+            "ltd,ldf->tlf",
+            lax.dynamic_slice_in_dim(mlp_inputs, start, part.shape[1], axis=2),
+            part,
+            preferred_element_type=jnp.float32,
+        ),
     )
     local_feats = jnp.maximum(pre_act + enc_bias[None, :, :], 0.0).astype(jnp.bfloat16)
     token_feats = lax.all_gather(local_feats, "width", axis=0, tiled=True)

time: 398 us -> 396 us (level)
  waiting for transfers between devices: 321 us -> 303 us
  starting transfers between devices: 4.52 us -> 17 us
    all_gather x1 -> x0, waiting for transfers between devices: 109 us -> none  [local(): lax.all_gather(encoder, 'width', axis=1, tiled=True)]
    ppermute x0 -> x7, waiting for transfers between devices: none -> 92.3 us  [the longest x4 92.3 us: report_classes(): lower = ppermute(lower, 'width', buffers)]
    ppermute x0 -> x7, starting transfers between devices: none -> 12 us  [the longest x3 9.45 us: report_classes(): d_next = ppermute(d_next, 'width', lanes)]
    dot_general x1 -> x8, matrix products: 7.31 us -> 9.79 us  [local(): jnp.einsum('ltd,ldf->tlf', lax.dynamic_slice_in_dim(mlp_inputs, start, pa...]
  transfers between devices with their start and end apart: 4 -> 10, of which waited for: 4 -> 7; matrix products, arithmetic and copies ran while one was open for 0% -> 2% of each run, Pallas kernels for 0% -> 0%
where the time goes in v1:
time: 396 us; the launch traced here: 395 us
  waiting for transfers between devices  303 us (77%)
  matrix products  29.2 us (7%)
  between operations  27.3 us (7%)
  starting transfers between devices  17 us (4%)
  local copies, waits for them, and re-layouts  15.6 us (4%)
    psum x1, waiting for transfers between devices, local(): summed = lax.psum(rebuilt, ('section', 'feat'))  123 us
    ppermute x4, waiting for transfers between devices, report_classes(): lower = ppermute(lower, 'width', buffers)  92.3 us
    all_gather x1, waiting for transfers between devices, local(): token_feats = lax.all_gather(local_feats, 'width', axis=0, tiled=True)  57 us
    ppermute x1, waiting for transfers between devices, from_behind(): lax.ppermute(value, axis, [(source, source + steps) for source in range(i...  30.3 us
    dot_general x5, matrix products, local(): jnp.dot(picked, decoder[pair_slot], preferred_element_type=jnp.float32)  13.5 us
    dot_general x8, matrix products, local(): jnp.einsum('ltd,ldf->tlf', lax.dynamic_slice_in_dim(mlp_inputs, start, pa...  9.79 us
    ppermute x3, starting transfers between devices, report_classes(): d_next = ppermute(d_next, 'width', lanes)  9.45 us
  transfers between devices with their start and end apart: 10, of which 7 were waited for; matrix products, arithmetic and copies ran while one was open for 2% of the time, Pallas kernels for 0%

profile of v1, /device:TPU:1, one launch (start us, length us, event | category | flops | bytes accessed | tf_op | source)
XLA Modules:
  0.0 395.5 jit_solution(12592207837010925702)
XLA Ops:
  7.2 0.0 copy-start
  7.2 0.0 all-gather.2.cloned.1.call-start
  7.2 2.5 collective-permute-start.1
  9.8 4.0 %collective-permute-start = (bf16[2,288,1024]{2,1,0:T(8,128)(2,1)}, bf16[2,288,1024]{2,1,0:T(8,128)(2,1)}, u32[]{:S(2)}, u32[]{:S(2)}) collective-permute-start(bf16[2,288,1024]{2,1,0:T(8,128)(2,1)} %param.10), channel_id=1, source_target_pairs={{0,7},{1,0},{2,1},{3,2},{4,3},{5,4},{6,5},{7,6},{8,15},{9,8},{10,9... | collective-permute-start | bytes 3538952 | tf_op jit(solution)/shard_map/ppermute | solution.py:22
  13.8 25.8 %collective-permute-done.1 = bf16[2,288,1024]{2,1,0:T(8,128)(2,1)S(1)} collective-permute-done((bf16[2,288,1024]{2,1,0:T(8,128)(2,1)}, bf16[2,288,1024]{2,1,0:T(8,128)(2,1)S(1)}, u32[]{:S(2)}, u32[]{:S(2)}) %collective-permute-start.1) | collective-permute-done | bytes 1179680 | tf_op jit(solution)/shard_map/ppermute | solution.py:20
  39.6 2.7 collective-permute-start.2
  42.3 24.9 %collective-permute-done.3 = bf16[2,288,1024]{2,1,0:T(8,128)(2,1)} collective-permute-done((bf16[2,288,1024]{2,1,0:T(8,128)(2,1)S(1)}, bf16[2,288,1024]{2,1,0:T(8,128)(2,1)}, u32[]{:S(2)}, u32[]{:S(2)}) %collective-permute-start.3) | collective-permute-done | bytes 1179680 | tf_op jit(solution)/shard_map/ppermute | solution.py:20
  67.2 1.7 fusion.69
  68.9 1.8 convolution_add_fusion.8
  70.7 2.8 collective-permute-start.4
  73.5 0.5 convolution_add_fusion.7
  74.0 20.2 %collective-permute-done.5 = bf16[2,288,1024]{2,1,0:T(8,128)(2,1)} collective-permute-done((bf16[2,288,1024]{2,1,0:T(8,128)(2,1)}, bf16[2,288,1024]{2,1,0:T(8,128)(2,1)}, u32[]{:S(2)}, u32[]{:S(2)}) %collective-permute-start.5) | collective-permute-done | bytes 1179680 | tf_op jit(solution)/shard_map/ppermute | solution.py:20
  94.1 1.8 fusion.64
  95.9 0.5 fusion.19
  96.4 1.8 fusion.61
  98.2 0.5 fusion.20
  98.7 21.4 %collective-permute-done.6 = bf16[2,288,1024]{2,1,0:T(8,128)(2,1)S(1)} collective-permute-done((bf16[2,288,1024]{2,1,0:T(8,128)(2,1)}, bf16[2,288,1024]{2,1,0:T(8,128)(2,1)S(1)}, u32[]{:S(2)}, u32[]{:S(2)}) %collective-permute-start.6) | collective-permute-done | bytes 1179680 | tf_op jit(solution)/shard_map/ppermute | solution.py:20
  120.1 1.3 fusion.39
  121.4 0.0 all-gather.2.cloned.1.call-update
  121.4 0.0 copy-start.5
  121.4 0.0 all-reduce.2.cloned.1.call-start
  121.5 57.0 %all-gather.2.cloned.1.call-done = bf16[1024,2,1024]{2,0,1:T(8,128)(2,1)} async-done(((bf16[128,2,1024]{2,0,1:T(8,128)(2,1)}), bf16[1024,2,1024]{2,0,1:T(8,128)(2,1)}) %all-gather.2.cloned.1.call-update) | async-done | bytes 4194320 | tf_op jit(solution)/shard_map/all_gather | solution.py:56
  178.5 3.1 slice_bitcast_fusion
  181.6 4.9 %collective-permute-start.7 = (bf16[1024,1024]{1,0:T(8,128)(2,1)}, bf16[1024,1024]{1,0:T(8,128)(2,1)S(1)}, u32[]{:S(2)}, u32[]{:S(2)}) collective-permute-start(bf16[1024,1024]{1,0:T(8,128)(2,1)} %slice_bitcast_fusion), channel_id=1, source_target_pairs={{0,128},{1,129},{2,130},{3,131},{4,132},{5,133},{6,134},{7,135},{8... | collective-permute-start | bytes 6291464 | tf_op jit(solution)/shard_map/ppermute | solution.py:31
  186.6 0.7 fusion.94
  200.3 30.3 %collective-permute-done.7 = bf16[1024,1024]{1,0:T(8,128)(2,1)S(1)} collective-permute-done((bf16[1024,1024]{1,0:T(8,128)(2,1)}, bf16[1024,1024]{1,0:T(8,128)(2,1)S(1)}, u32[]{:S(2)}, u32[]{:S(2)}) %collective-permute-start.7) | collective-permute-done | bytes 2097184 | tf_op jit(solution)/shard_map/ppermute | solution.py:31
  230.7 3.0 broadcast_in_dim.25
  233.6 0.8 copy-done.1
  234.5 3.6 fusion.18
  238.1 1.3 constant_dynamic-slice_fusion.3
  239.4 2.4 fusion.17
  241.9 1.3 constant_dynamic-slice_fusion.2
  243.2 2.5 fusion.15
  245.7 1.3 constant_dynamic-slice_fusion.1
  247.0 2.5 fusion.13
  249.5 1.3 constant_dynamic-slice_fusion
  250.9 2.5 fusion.11
  253.4 0.0 all-reduce.2.cloned.1.call-update
  253.4 0.7 copy-done.9
  254.0 122.8 %all-reduce.2.cloned.1.call-done = f32[4,1024,288]{1,2,0:T(8,128)} async-done(((f32[4,1024,288]{1,2,0:T(8,128)}), f32[4,1024,288]{1,2,0:T(8,128)}) %all-reduce.2.cloned.1.call-update) | async-done | bytes 4718608 | tf_op jit(solution)/shard_map/psum | solution.py:76
  376.8 3.9 multiply_convert_fusion
  380.8 0.3 copy-done.2
  381.1 1.2 fusion.38
  382.3 1.2 fusion.36
  383.4 1.2 fusion.34
  384.6 1.2 fusion.32
  385.8 1.2 fusion.30
  387.0 1.6 copy-done.10
  (23 shorter events, 0.1 us)
Async XLA Ops:
  7.2 60.0 %copy-start = (bf16[2,128,2304]{2,1,0:T(8,128)(2,1)S(1)}, bf16[2,128,2304]{2,1,0:T(8,128)(2,1)}, u32[]{:S(2)}) copy-start(bf16[2,128,2304]{2,1,0:T(8,128)(2,1)} %param.9) | copy-start | bytes 3538948
  7.2 171.4 %all-gather.2.cloned.1.call-start = ((), (), s32[]{:S(2)}) async-start(), calls=%async_computation | async-start | bytes 4718592 | tf_op jit(solution)/shard_map/all_gather | solution.py:56
  7.2 32.4 %collective-permute-start.1 = (bf16[2,288,1024]{2,1,0:T(8,128)(2,1)}, bf16[2,288,1024]{2,1,0:T(8,128)(2,1)S(1)}, u32[]{:S(2)}, u32[]{:S(2)}) collective-permute-start(bf16[2,288,1024]{2,1,0:T(8,128)(2,1)} %param.10), channel_id=1, source_target_pairs={{0,1},{1,2},{2,3},{3,4},{4,5},{5,6},{6,7},{7,0},{8,9},{9,10},{10,1... | collective-permute-start | bytes 3538952 | tf_op jit(solution)/shard_map/ppermute | solution.py:20
  9.8 29.8 %collective-permute-start = (bf16[2,288,1024]{2,1,0:T(8,128)(2,1)}, bf16[2,288,1024]{2,1,0:T(8,128)(2,1)}, u32[]{:S(2)}, u32[]{:S(2)}) collective-permute-start(bf16[2,288,1024]{2,1,0:T(8,128)(2,1)} %param.10), channel_id=1, source_target_pairs={{0,7},{1,0},{2,1},{3,2},{4,3},{5,4},{6,5},{7,6},{8,15},{9,8},{10,9... | collective-permute-start | bytes 3538952 | tf_op jit(solution)/shard_map/ppermute | solution.py:22
  39.6 27.6 %collective-permute-start.3 = (bf16[2,288,1024]{2,1,0:T(8,128)(2,1)S(1)}, bf16[2,288,1024]{2,1,0:T(8,128)(2,1)}, u32[]{:S(2)}, u32[]{:S(2)}) collective-permute-start(bf16[2,288,1024]{2,1,0:T(8,128)(2,1)S(1)} %collective-permute-done.1), channel_id=1, source_target_pairs={{0,1},{1,2},{2,3},{3,4},{4,5},{5,6},{6,7},{7,0},{8,9},{9,10},{10,1... | collective-permute-start | bytes 3538952 | tf_op jit(solution)/shard_map/ppermute | solution.py:20
  39.6 31.1 %collective-permute-start.2 = (bf16[2,288,1024]{2,1,0:T(8,128)(2,1)}, bf16[2,288,1024]{2,1,0:T(8,128)(2,1)S(1)}, u32[]{:S(2)}, u32[]{:S(2)}) collective-permute-start(bf16[2,288,1024]{2,1,0:T(8,128)(2,1)} %collective-permute-done), channel_id=1, source_target_pairs={{0,7},{1,0},{2,1},{3,2},{4,3},{5,4},{6,5},{7,6},{8,15},{9,8},{10,9... | collective-permute-start | bytes 3538952 | tf_op jit(solution)/shard_map/ppermute | solution.py:22
  67.2 26.9 %collective-permute-start.5 = (bf16[2,288,1024]{2,1,0:T(8,128)(2,1)}, bf16[2,288,1024]{2,1,0:T(8,128)(2,1)}, u32[]{:S(2)}, u32[]{:S(2)}) collective-permute-start(bf16[2,288,1024]{2,1,0:T(8,128)(2,1)} %collective-permute-done.3), channel_id=1, source_target_pairs={{0,1},{1,2},{2,3},{3,4},{4,5},{5,6},{6,7},{7,0},{8,9},{9,10},{10,1... | collective-permute-start | bytes 3538952 | tf_op jit(solution)/shard_map/ppermute | solution.py:20
  70.7 27.5 %collective-permute-start.4 = (bf16[2,288,1024]{2,1,0:T(8,128)(2,1)S(1)}, bf16[2,288,1024]{2,1,0:T(8,128)(2,1)S(1)}, u32[]{:S(2)}, u32[]{:S(2)}) collective-permute-start(bf16[2,288,1024]{2,1,0:T(8,128)(2,1)S(1)} %collective-permute-done.2), channel_id=1, source_target_pairs={{0,7},{1,0},{2,1},{3,2},{4,3},{5,4},{6,5},{7,6},{8,15},{9,8},{10,9... | collective-permute-start | bytes 3538952 | tf_op jit(solution)/shard_map/ppermute | solution.py:22
  94.1 26.0 %collective-permute-start.6 = (bf16[2,288,1024]{2,1,0:T(8,128)(2,1)}, bf16[2,288,1024]{2,1,0:T(8,128)(2,1)S(1)}, u32[]{:S(2)}, u32[]{:S(2)}) collective-permute-start(bf16[2,288,1024]{2,1,0:T(8,128)(2,1)} %collective-permute-done.5), channel_id=1, source_target_pairs={{0,1},{1,2},{2,3},{3,4},{4,5},{5,6},{6,7},{7,0},{8,9},{9,10},{10,1... | collective-permute-start | bytes 3538952 | tf_op jit(solution)/shard_map/ppermute | solution.py:20
  98.2 21.9 %copy-start.7 = (f32[2,1024]{1,0:T(2,128)S(1)}, f32[2,1024]{1,0:T(2,128)}, u32[]{:S(2)}) copy-start(f32[2,1024]{1,0:T(2,128)} %param.11) | copy-start | bytes 24580
  121.4 65.1 %copy-start.5 = (s32[10]{0:T(128)S(1)}, s32[10]{0:T(128)}, u32[]{:S(2)}) copy-start(s32[10]{0:T(128)} %constant.142.clone) | copy-start | bytes 124
  121.4 65.1 %copy-start.6 = (s32[10]{0:T(128)S(1)}, s32[10]{0:T(128)}, u32[]{:S(2)}) copy-start(s32[10]{0:T(128)} %constant.143.clone) | copy-start | bytes 124
  121.4 255.4 %all-reduce.2.cloned.1.call-start = ((), (), s32[]{:S(2)}) async-start(), calls=%async_computation.1 | async-start | bytes 9437184 | tf_op jit(solution)/shard_map/psum | solution.py:76
  181.6 49.0 %collective-permute-start.7 = (bf16[1024,1024]{1,0:T(8,128)(2,1)}, bf16[1024,1024]{1,0:T(8,128)(2,1)S(1)}, u32[]{:S(2)}, u32[]{:S(2)}) collective-permute-start(bf16[1024,1024]{1,0:T(8,128)(2,1)} %slice_bitcast_fusion), channel_id=1, source_target_pairs={{0,128},{1,129},{2,130},{3,131},{4,132},{5,133},{6,134},{7,135},{8... | collective-permute-start | bytes 6291464 | tf_op jit(solution)/shard_map/ppermute | solution.py:31
  230.7 3.8 copy-start.1
  234.5 5.0 %copy-start.4 = (bf16[5,1024,288]{1,2,0:T(8,128)(2,1)S(1)}, bf16[5,1024,288]{1,2,0:T(8,128)(2,1)}, u32[]{:S(2)}) copy-start(bf16[5,1024,288]{1,2,0:T(8,128)(2,1)} %param.12) | copy-start | bytes 8847364
  253.4 0.7 copy-start.9
  253.4 123.5 %copy-start.8 = (f32[4,288]{1,0:T(4,128)S(1)}, f32[4,288]{1,0:T(4,128)}, u32[]{:S(2)}) copy-start(f32[4,288]{1,0:T(4,128)} %param.13) | copy-start | bytes 13828
  376.8 4.2 %copy-start.2 = (bf16[1024,2,1024]{2,0,1:T(8,128)(2,1)S(1)}, bf16[1024,2,1024]{2,0,1:T(8,128)(2,1)}, u32[]{:S(2)}) copy-start(bf16[1024,2,1024]{2,0,1:T(8,128)(2,1)} %all-gather.2.cloned.1.call-done) | copy-start | bytes 12582916
  381.1 4.7 %copy-start.3 = (bf16[4,1024,288]{1,2,0:T(8,128)(2,1)}, bf16[4,1024,288]{1,2,0:T(8,128)(2,1)S(1)}, u32[]{:S(2)}) copy-start(bf16[4,1024,288]{1,2,0:T(8,128)(2,1)S(1)} %multiply_convert_fusion) | copy-start | bytes 7077892
  387.0 1.6 copy-start.10
Sparse Core Ops, SparseCore 0:
  121.5 56.9 all-gather.1
  253.5 123.2 all-reduce.1
